TPU v7x, 256 devices: a whole 4x4x8 slice. The times are simulated.
256 devices in a mesh: freq: 8 (over y, x_hi), rec: 32 (over x_lo, z, core).
Axes of the slice: x: 4 (x_hi: 2, x_lo: 2; x = x_hi * 2 + x_lo), y: 4, z: 8, core: 2. Of those that a mesh axis runs over, the one named last changes fastest.
Arguments:
- response: bfloat16 [128, 2, 1792, 1792], P('freq', None, 'rec'), may hold values from -1 to 1, as said below
- direct: float32 [1792, 32, 256], P('rec', 'freq'), may hold values from -6 to 6
- onset: int32 [1792, 32], P('rec', 'freq'), may hold values from 16 to 128
Outputs:
- upgoing: float32 [1792, 32, 256], P('rec', 'freq')
- coda: float32 [1792, 32, 256], P('rec', 'freq')
Inputs may be any that keep to these rules, and one draw needn't show every extreme that they name: response[k, c, r, s] = response[k, c, s, r] for every frequency and part (source-receiver reciprocity).
All inputs are finite; a program needn't handle non-finite values.
Results may differ from a plain program's by a relative error of at most 0.023.
Values may be sent and summed in bfloat16 or wider, within the bound.
A program may use at most 128 MiB of HBM per device.

v0:
```python
import math
import jax
import jax.numpy as jnp
from jax import lax
from jax.sharding import PartitionSpec as P

NF = 128
NT = 256
ITERS = 2


def spectral_tables(length, count):
    samples = jnp.arange(length, dtype=jnp.int32)
    frequency_bins = jnp.arange(1, count + 1, dtype=jnp.int32)
    phase = (samples[:, None] * frequency_bins[None, :] % length).astype(jnp.float32) * (
        2.0 * math.pi / length
    )
    cosine = jnp.cos(phase)
    sine = jnp.sin(phase)
    forward = jnp.stack([cosine, -sine], axis=1)
    inverse = jnp.stack([cosine.T, -sine.T], axis=0) * (2.0 / length)
    return (forward, inverse)


def make_window(onset, length):
    samples = jnp.arange(length, dtype=jnp.int32)
    folded = jnp.minimum(samples, length - samples)
    return (folded[None, None, :] < onset[:, :, None]).astype(jnp.float32)


def to_spectrum(field, forward):
    packed = jnp.einsum("svt,tck->kcvs", field, forward)
    return packed.astype(jnp.bfloat16)


def to_time(spectra, inverse):
    return jnp.einsum("kcvs,ckt->svt", spectra.astype(jnp.float32), inverse)


def complex_apply(block, spectra, conj_sign):
    parts = jnp.einsum("fcrs,fdvs->cdfvr", block, spectra, preferred_element_type=jnp.float32)
    real_out = parts[0, 0] - conj_sign * parts[1, 1]
    imag_out = parts[0, 1] + conj_sign * parts[1, 0]
    return jnp.stack([real_out, imag_out], axis=1)


def body(response, direct, onset):
    forward, inverse = spectral_tables(NT, NF)
    window = make_window(onset, NT)
    coda = jnp.zeros_like(direct)
    upgoing = coda
    for iteration in range(ITERS):
        downgoing = direct + coda
        sources = lax.all_to_all(
            to_spectrum(downgoing, forward), "freq", split_axis=0, concat_axis=2, tiled=True
        )
        gathered = lax.all_gather(sources, "rec", axis=3, tiled=True)
        reflected = complex_apply(response, gathered, 1.0)
        reflected_time = lax.all_to_all(
            reflected.astype(jnp.bfloat16), "freq", split_axis=2, concat_axis=0, tiled=True
        )
        upgoing = window * to_time(reflected_time, inverse)
        spectra_up = lax.all_to_all(
            to_spectrum(upgoing, forward), "freq", split_axis=0, concat_axis=2, tiled=True
        )
        receivers = lax.all_gather(spectra_up, "rec", axis=3, tiled=True)
        returned = complex_apply(response, receivers, -1.0)
        returned_time = lax.all_to_all(
            returned.astype(jnp.bfloat16), "freq", split_axis=2, concat_axis=0, tiled=True
        )
        coda = window * to_time(returned_time, inverse)
    return (upgoing, coda)


def solution(mesh):
    placed = (P("freq", None, "rec", None), P("rec", "freq", None), P("rec", "freq"))
    return jax.shard_map(
        body,
        mesh=mesh,
        in_specs=placed,
        out_specs=(P("rec", "freq", None), P("rec", "freq", None)),
        check_vma=False,
    )
```

profile of v0, /device:TPU:96, one launch (start us, length us, event | category | flops | bytes accessed | tf_op | source)
XLA Modules:
  0.0 545.7 jit_solution(14085154062390279766)
XLA Ops:
  7.8 1.1 fusion.39
  9.5 14.9 %all_to_all.144 = bf16[8,2,3584]{2,1,0:T(2,128)(2,1)S(1)} all-to-all(bf16[8,2,3584]{2,1,0:T(2,128)(2,1)S(1)} %reshape.396), channel_id=1, replica_groups=mesh['freq'=8,'rec'=32] {'freq'}, dimensions={0} | all-to-all | bytes 229376 | tf_op jit(solution)/shard_map/all_to_all | solution.py:54
  24.9 1.5 copy.89
  27.0 87.4 %all-gather.5.cloned.1.call-done = bf16[16,2,32,1792]{2,0,1,3:T(8,128)(2,1)} async-done(((bf16[16,2,32,56]{2,0,1,3:T(8,128)(2,1)}), bf16[16,2,32,1792]{2,0,1,3:T(8,128)(2,1)}) %all-gather.5.cloned.1.call-update) | async-done | bytes 3670032 | tf_op jit(solution)/shard_map/all_gather | solution.py:57
  114.4 15.0 %fusion.17 = f32[2,2,16,32,56]{4,3,0,1,2:T(8,128)S(1)} fusion(bf16[16,2,56,1792]{3,2,1,0:T(8,128)(2,1)} %param.3, bf16[16,2,32,1792,1]{2,0,1,3,4:T(8,128)(2,1)} %bitcast.271), kind=kOutput, calls=%fused_computation.13 | convolution fusion | flops 411041792 | bytes 10551296 | tf_op jit(solution)/shard_map/fcrs,fdvs->cdfvr/dot_general | solution.py:41
  129.7 1.1 reshape.398
  130.8 6.7 %all-to-all-start.1 = ((bf16[8,2,3584]{2,1,0:T(2,128)(2,1)}), bf16[8,2,3584]{2,1,0:T(2,128)(2,1)S(1)}, u32[]{:S(2)}, u32[]{:S(2)}) async-start(bf16[8,2,3584]{2,1,0:T(2,128)(2,1)} %reshape.398), calls=%async_computation.1 | async-start | bytes 229376 | tf_op jit(solution)/shard_map/all_to_all | solution.py:59
  137.6 8.1 %all-to-all-done.1 = bf16[8,2,3584]{2,1,0:T(2,128)(2,1)S(1)} async-done(((bf16[8,2,3584]{2,1,0:T(2,128)(2,1)}), bf16[8,2,3584]{2,1,0:T(2,128)(2,1)S(1)}, u32[]{:S(2)}, u32[]{:S(2)}) %all-to-all-start.1) | async-done | bytes 114720 | tf_op jit(solution)/shard_map/all_to_all | solution.py:59
  147.1 10.5 %all_to_all.145 = bf16[8,2,3584]{2,1,0:T(2,128)(2,1)S(1)} all-to-all(bf16[8,2,3584]{2,1,0:T(2,128)(2,1)S(1)} %reshape.400), channel_id=1, replica_groups=mesh['freq'=8,'rec'=32] {'freq'}, dimensions={0} | all-to-all | bytes 229376 | tf_op jit(solution)/shard_map/all_to_all | solution.py:63
  158.2 1.5 copy.99
  159.9 85.8 %all-gather.7.cloned.1.call-done = bf16[16,2,32,1792]{2,0,1,3:T(8,128)(2,1)} async-done(((bf16[16,2,32,56]{2,0,1,3:T(8,128)(2,1)}), bf16[16,2,32,1792]{2,0,1,3:T(8,128)(2,1)}) %all-gather.7.cloned.1.call-update) | async-done | bytes 3670032 | tf_op jit(solution)/shard_map/all_gather | solution.py:66
  245.6 15.1 %fusion.22 = f32[2,2,16,32,56]{4,3,0,1,2:T(8,128)S(1)} fusion(bf16[16,2,56,1792]{3,2,1,0:T(8,128)(2,1)} %param.3, bf16[16,2,32,1792,1]{2,0,1,3,4:T(8,128)(2,1)} %bitcast.272), kind=kOutput, calls=%fused_computation.14 | convolution fusion | flops 411041792 | bytes 10551296 | tf_op jit(solution)/shard_map/fcrs,fdvs->cdfvr/dot_general | solution.py:41
  261.4 14.6 %all_to_all.146 = bf16[8,2,3584]{2,1,0:T(2,128)(2,1)S(1)} all-to-all(bf16[8,2,3584]{2,1,0:T(2,128)(2,1)S(1)} %reshape.402), channel_id=1, replica_groups=mesh['freq'=8,'rec'=32] {'freq'}, dimensions={0} | all-to-all | bytes 229376 | tf_op jit(solution)/shard_map/all_to_all | solution.py:68
  277.5 10.5 %all_to_all.147 = bf16[8,2,3584]{2,1,0:T(2,128)(2,1)S(1)} all-to-all(bf16[8,2,3584]{2,1,0:T(2,128)(2,1)S(1)} %reshape.404), channel_id=1, replica_groups=mesh['freq'=8,'rec'=32] {'freq'}, dimensions={0} | all-to-all | bytes 229376 | tf_op jit(solution)/shard_map/all_to_all | solution.py:54
  288.6 1.5 copy.111
  290.3 85.7 %all-gather.9.cloned.1.call-done = bf16[16,2,32,1792]{2,0,1,3:T(8,128)(2,1)} async-done(((bf16[16,2,32,56]{2,0,1,3:T(8,128)(2,1)}), bf16[16,2,32,1792]{2,0,1,3:T(8,128)(2,1)}) %all-gather.9.cloned.1.call-update) | async-done | bytes 3670032 | tf_op jit(solution)/shard_map/all_gather | solution.py:57
  376.0 15.0 %fusion.27 = f32[2,2,16,32,56]{4,3,0,1,2:T(8,128)S(1)} fusion(bf16[16,2,56,1792]{3,2,1,0:T(8,128)(2,1)} %param.3, bf16[16,2,32,1792,1]{2,0,1,3,4:T(8,128)(2,1)} %bitcast.273), kind=kOutput, calls=%fused_computation.15 | convolution fusion | flops 411041792 | bytes 10551296 | tf_op jit(solution)/shard_map/fcrs,fdvs->cdfvr/dot_general | solution.py:41
  391.8 14.6 %all_to_all.148 = bf16[8,2,3584]{2,1,0:T(2,128)(2,1)S(1)} all-to-all(bf16[8,2,3584]{2,1,0:T(2,128)(2,1)S(1)} %reshape.406), channel_id=1, replica_groups=mesh['freq'=8,'rec'=32] {'freq'}, dimensions={0} | all-to-all | bytes 229376 | tf_op jit(solution)/shard_map/all_to_all | solution.py:59
  407.9 10.5 %all_to_all.149 = bf16[8,2,3584]{2,1,0:T(2,128)(2,1)S(1)} all-to-all(bf16[8,2,3584]{2,1,0:T(2,128)(2,1)S(1)} %reshape.408), channel_id=1, replica_groups=mesh['freq'=8,'rec'=32] {'freq'}, dimensions={0} | all-to-all | bytes 229376 | tf_op jit(solution)/shard_map/all_to_all | solution.py:63
  419.0 1.5 copy.121
  420.5 86.0 %all-gather.11.cloned.1.call-done = bf16[16,2,32,1792]{2,0,1,3:T(8,128)(2,1)} async-done(((bf16[16,2,32,56]{2,0,1,3:T(8,128)(2,1)}), bf16[16,2,32,1792]{2,0,1,3:T(8,128)(2,1)}) %all-gather.11.cloned.1.call-update) | async-done | bytes 3670032 | tf_op jit(solution)/shard_map/all_gather | solution.py:66
  506.5 15.0 %fusion.12 = f32[2,2,16,32,56]{4,3,2,1,0:T(8,128)S(1)} fusion(bf16[16,2,32,1792,1]{2,0,1,3,4:T(8,128)(2,1)} %bitcast.274, bf16[16,2,56,1792]{3,2,1,0:T(8,128)(2,1)} %param.3), kind=kOutput, calls=%fused_computation.12 | convolution fusion | flops 411041792 | bytes 10551296 | tf_op jit(solution)/shard_map/fcrs,fdvs->cdfvr/dot_general | solution.py:41
  522.8 6.7 %all-to-all-start.7 = ((bf16[8,2,3584]{2,1,0:T(2,128)(2,1)}), bf16[8,2,3584]{2,1,0:T(2,128)(2,1)S(1)}, u32[]{:S(2)}, u32[]{:S(2)}) async-start(bf16[8,2,3584]{2,1,0:T(2,128)(2,1)} %reshape.410), calls=%async_computation.7 | async-start | bytes 229376 | tf_op jit(solution)/shard_map/all_to_all | solution.py:68
  530.3 7.4 %all-to-all-done.7 = bf16[8,2,3584]{2,1,0:T(2,128)(2,1)S(1)} async-done(((bf16[8,2,3584]{2,1,0:T(2,128)(2,1)}), bf16[8,2,3584]{2,1,0:T(2,128)(2,1)S(1)}, u32[]{:S(2)}, u32[]{:S(2)}) %all-to-all-start.7) | async-done | bytes 114720 | tf_op jit(solution)/shard_map/all_to_all | solution.py:68
  (69 shorter events, 13.9 us)
Async XLA Ops:
  7.2 107.3 %all-gather.5.cloned.1.call-start = ((), (), s32[]{:S(2)}) async-start(), calls=%async_computation.8 | async-start | bytes 15138816 | tf_op jit(solution)/shard_map/all_gather | solution.py:57
  114.4 31.7 %copy-start.1 = (s32[56,4]{0,1:T(4,128)S(1)}, s32[56,4]{0,1:T(4,128)}, u32[]{:S(2)}) copy-start(s32[56,4]{0,1:T(4,128)} %param.5) | copy-start | bytes 2692
  130.8 14.8 %all-to-all-start.1 = ((bf16[8,2,3584]{2,1,0:T(2,128)(2,1)}), bf16[8,2,3584]{2,1,0:T(2,128)(2,1)S(1)}, u32[]{:S(2)}, u32[]{:S(2)}) async-start(bf16[8,2,3584]{2,1,0:T(2,128)(2,1)} %reshape.398), calls=%async_computation.1 | async-start | bytes 229376 | tf_op jit(solution)/shard_map/all_to_all | solution.py:59
  137.5 108.1 %all-gather.7.cloned.1.call-start = ((), (), s32[]{:S(2)}) async-start(), calls=%async_computation.9 | async-start | bytes 15138816 | tf_op jit(solution)/shard_map/all_gather | solution.py:66
  159.6 216.4 %all-gather.9.cloned.1.call-start = ((), (), s32[]{:S(2)}) async-start(), calls=%async_computation.10 | async-start | bytes 15138816 | tf_op jit(solution)/shard_map/all_gather | solution.py:57
  245.6 30.9 %copy-start = (f32[56,4,256]{2,1,0:T(4,128)S(1)}, f32[56,4,256]{2,1,0:T(4,128)}, u32[]{:S(2)}) copy-start(f32[56,4,256]{2,1,0:T(4,128)} %param.4) | copy-start | bytes 688132
  290.1 216.4 %all-gather.11.cloned.1.call-start = ((), (), s32[]{:S(2)}) async-start(), calls=%async_computation.11 | async-start | bytes 15138816 | tf_op jit(solution)/shard_map/all_gather | solution.py:66
  522.8 14.8 %all-to-all-start.7 = ((bf16[8,2,3584]{2,1,0:T(2,128)(2,1)}), bf16[8,2,3584]{2,1,0:T(2,128)(2,1)S(1)}, u32[]{:S(2)}, u32[]{:S(2)}) async-start(bf16[8,2,3584]{2,1,0:T(2,128)(2,1)} %reshape.410), calls=%async_computation.7 | async-start | bytes 229376 | tf_op jit(solution)/shard_map/all_to_all | solution.py:68
Sparse Core Ops, SparseCore 0:
  26.5 87.8 all-gather.4
  159.8 85.8 all-gather.6
  290.2 85.8 all-gather.8
  420.6 85.8 all-gather.10
where the time goes:
time: 546 us
  waiting for transfers between devices  360 us (66%)
  blocking collectives  75.7 us (14%)
  matrix products  62.6 us (11%)
  local copies, waits for them, and re-layouts  17 us (3%)
  between operations  14.2 us (3%)
  starting transfers between devices  14 us (3%)
    all_gather x2, waiting for transfers between devices, body(): gathered = lax.all_gather(sources, 'rec', axis=3, tiled=True)  173 us
    all_gather x2, waiting for transfers between devices, body(): receivers = lax.all_gather(spectra_up, 'rec', axis=3, tiled=True)  172 us
    dot_general x4, matrix products, complex_apply(): jnp.einsum('fcrs,fdvs->cdfvr', block, spectra, preferred_element_type=jnp...  60.1 us
    all_to_all x2, blocking collectives, body(): lax.all_to_all(to_spectrum(downgoing, forward), 'freq', split_axis=0, con...  25.4 us
    all_to_all x2, blocking collectives, body(): lax.all_to_all(to_spectrum(upgoing, forward), 'freq', split_axis=0, conca...  21.1 us
    all_to_all x1, blocking collectives, body(): lax.all_to_all(reflected.astype(jnp.bfloat16), 'freq', split_axis=2, conc...  14.6 us
    all_to_all x1, blocking collectives, body(): lax.all_to_all(returned.astype(jnp.bfloat16), 'freq', split_axis=2, conca...  14.6 us
  transfers between devices with their start and end apart: 6, of which 6 were waited for; matrix products, arithmetic and copies ran while one was open for 0% of the time, Pallas kernels for 0%

commit v1 on v0

--- a/solution.py
+++ b/solution.py
@@ -54,7 +54,9 @@
         sources = lax.all_to_all(
             to_spectrum(downgoing, forward), "freq", split_axis=0, concat_axis=2, tiled=True
         )
-        gathered = lax.all_gather(sources, "rec", axis=3, tiled=True)
+        gathered = jnp.concatenate(
+            lax.all_to_all(jnp.stack([sources] * lax.axis_size("rec")), "rec", 0, 0), axis=3
+        )
         reflected = complex_apply(response, gathered, 1.0)
         reflected_time = lax.all_to_all(
             reflected.astype(jnp.bfloat16), "freq", split_axis=2, concat_axis=0, tiled=True

time: 546 us -> 698 us (1.28); the launches traced: 546 us -> 690 us
  local copies, waits for them, and re-layouts: 17 us -> 176 us
  waiting for transfers between devices: 360 us -> 271 us
  blocking collectives: 75.7 us -> 161 us
  matrix products: 62.6 us -> 47.6 us
    all_gather x2 -> x0, waiting for transfers between devices: 173 us -> none  [body(): gathered = lax.all_gather(sources, 'rec', axis=3, tiled=True)]
    all_to_all x0 -> x1, blocking collectives: none -> 88.9 us  [body(): lax.all_to_all(jnp.stack([sources] * lax.axis_size('rec')), 'rec', 0, 0)]
    all_to_all x0 -> x1, waiting for transfers between devices: none -> 84.2 us  [body(): lax.all_to_all(jnp.stack([sources] * lax.axis_size('rec')), 'rec', 0, 0)]
    unnamed x22 -> x26, local copies, waits for them, and re-layouts: 9.64 us -> 91.8 us
    reshape x0 -> x4, local copies, waits for them, and re-layouts: none -> 68.5 us  [body(): jnp.concatenate(lax.all_to_all(jnp.stack([sources] * lax.axis_size('rec')...]
    dot_general x4, matrix products: 60.1 us -> 45.1 us  [complex_apply(): jnp.einsum('fcrs,fdvs->cdfvr', block, spectra, preferred_element_type=jnp...]
    another operation x0 -> x4, local copies, waits for them, and re-layouts: none -> 10.9 us  [body(): jnp.stack([sources] * lax.axis_size('rec'))]
    all_to_all x0 -> x1, starting transfers between devices: none -> 7.9 us  [body(): lax.all_to_all(jnp.stack([sources] * lax.axis_size('rec')), 'rec', 0, 0)]
  transfers between devices with their start and end apart: 6 -> 5, of which waited for: 6 -> 5; matrix products, arithmetic and copies ran while one was open for 0% -> 0% of each run, Pallas kernels for 0% -> 0%
where the time goes in v1:
time: 698 us; the launch traced here: 690 us
  waiting for transfers between devices  271 us (39%)
  local copies, waits for them, and re-layouts  176 us (25%)
  blocking collectives  161 us (23%)
  matrix products  47.6 us (7%)
  starting transfers between devices  18 us (3%)
  between operations  14.7 us (2%)
    all_gather x2, waiting for transfers between devices, body(): receivers = lax.all_gather(spectra_up, 'rec', axis=3, tiled=True)  172 us
    unnamed x26, local copies, waits for them, and re-layouts  91.8 us
    all_to_all x1, blocking collectives, body(): lax.all_to_all(jnp.stack([sources] * lax.axis_size('rec')), 'rec', 0, 0)  88.9 us
    all_to_all x1, waiting for transfers between devices, body(): lax.all_to_all(jnp.stack([sources] * lax.axis_size('rec')), 'rec', 0, 0)  84.2 us
    reshape x4, local copies, waits for them, and re-layouts, body(): jnp.concatenate(lax.all_to_all(jnp.stack([sources] * lax.axis_size('rec')...  68.5 us
    dot_general x4, matrix products, complex_apply(): jnp.einsum('fcrs,fdvs->cdfvr', block, spectra, preferred_element_type=jnp...  45.1 us
    all_to_all x2, blocking collectives, body(): lax.all_to_all(to_spectrum(downgoing, forward), 'freq', split_axis=0, con...  25.4 us
    all_to_all x2, blocking collectives, body(): lax.all_to_all(to_spectrum(upgoing, forward), 'freq', split_axis=0, conca...  21.2 us
  transfers between devices with their start and end apart: 5, of which 5 were waited for; matrix products, arithmetic and copies ran while one was open for 0% of the time, Pallas kernels for 0%

profile of v1, /device:TPU:96, one launch (start us, length us, event | category | flops | bytes accessed | tf_op | source)
XLA Modules:
  0.0 689.6 jit_solution(9815836827543083634)
XLA Ops:
  9.5 14.9 %all_to_all.148 = bf16[8,2,3584]{2,1,0:T(2,128)(2,1)S(1)} all-to-all(bf16[8,2,3584]{2,1,0:T(2,128)(2,1)S(1)} %reshape.420), channel_id=1, replica_groups=mesh['freq'=8,'rec'=32] {'freq'}, dimensions={0} | all-to-all | bytes 229376 | tf_op jit(solution)/shard_map/all_to_all | solution.py:54
  30.3 19.8 %reshape.422 = bf16[32,2,28672]{2,1,0:T(2,128)(2,1)} reshape(bf16[32,16,2,32,56]{4,3,2,1,0:T(8,128)(2,1)} %stack.27) | data formatting | bytes 7340032
  50.1 7.9 %all-to-all-start.1 = ((bf16[32,2,28672]{2,1,0:T(2,128)(2,1)}), bf16[32,2,28672]{2,1,0:T(2,128)(2,1)}, u32[]{:S(2)}, u32[]{:S(2)}) async-start(bf16[32,2,28672]{2,1,0:T(2,128)(2,1)} %reshape.422), calls=%async_computation.1 | async-start | bytes 7340032 | tf_op jit(solution)/shard_map/all_to_all | solution.py:58
  58.6 84.2 %all-to-all-done.1 = bf16[32,2,28672]{2,1,0:T(2,128)(2,1)} async-done(((bf16[32,2,28672]{2,1,0:T(2,128)(2,1)}), bf16[32,2,28672]{2,1,0:T(2,128)(2,1)}, u32[]{:S(2)}, u32[]{:S(2)}) %all-to-all-start.1) | async-done | bytes 3670048 | tf_op jit(solution)/shard_map/all_to_all | solution.py:58
  142.8 21.3 %reshape.423 = bf16[32,16,2,32,56]{4,3,2,1,0:T(8,128)(2,1)} reshape(bf16[32,2,28672]{2,1,0:T(2,128)(2,1)} %all-to-all-done.1) | data formatting | bytes 7340032
  164.1 20.0 %copy.94 = bf16[16,2,32,32,56]{4,3,2,1,0:T(8,128)(2,1)} copy(bf16[16,2,32,32,56]{4,2,1,0,3:T(8,128)(2,1)} %bitcast.265) | data formatting | bytes 7340032 | tf_op jit(solution)/shard_map/reshape | solution.py:57
  184.1 14.3 %reshape.405 = bf16[16,2,32,1792,1]{3,2,1,0,4:T(8,128)(2,1)} reshape(bf16[16,2,32,32,56]{4,3,2,1,0:T(8,128)(2,1)} %copy.94) | data formatting | bytes 7340032 | tf_op jit(solution)/shard_map/reshape | solution.py:57
  198.3 7.4 %fusion.17 = f32[2,2,16,32,56]{4,3,0,1,2:T(8,128)S(1)} fusion(bf16[16,2,56,1792]{3,2,1,0:T(8,128)(2,1)} %param.3, bf16[16,2,32,1792,1]{3,2,1,0,4:T(8,128)(2,1)} %reshape.405), kind=kOutput, calls=%fused_computation.13 | convolution fusion | flops 411041792 | bytes 10551296 | tf_op jit(solution)/shard_map/fcrs,fdvs->cdfvr/dot_general | solution.py:41
  210.5 8.0 %all-to-all-done.2 = bf16[8,2,3584]{2,1,0:T(2,128)(2,1)S(1)} async-done(((bf16[8,2,3584]{2,1,0:T(2,128)(2,1)}), bf16[8,2,3584]{2,1,0:T(2,128)(2,1)S(1)}, u32[]{:S(2)}, u32[]{:S(2)}) %all-to-all-start.2) | async-done | bytes 114720 | tf_op jit(solution)/shard_map/all_to_all | solution.py:61
  219.9 10.5 %all_to_all.149 = bf16[8,2,3584]{2,1,0:T(2,128)(2,1)S(1)} all-to-all(bf16[8,2,3584]{2,1,0:T(2,128)(2,1)S(1)} %reshape.426), channel_id=1, replica_groups=mesh['freq'=8,'rec'=32] {'freq'}, dimensions={0} | all-to-all | bytes 229376 | tf_op jit(solution)/shard_map/all_to_all | solution.py:65
  232.5 85.8 %all-gather.3.cloned.1.call-done = bf16[16,2,32,1792]{2,0,1,3:T(8,128)(2,1)} async-done(((bf16[16,2,32,56]{2,0,1,3:T(8,128)(2,1)}), bf16[16,2,32,1792]{2,0,1,3:T(8,128)(2,1)}) %all-gather.3.cloned.1.call-update) | async-done | bytes 3670032 | tf_op jit(solution)/shard_map/all_gather | solution.py:68
  318.3 15.3 %fusion.27 = f32[2,2,16,32,56]{4,3,0,1,2:T(8,128)S(1)} fusion(bf16[16,2,56,1792]{3,2,1,0:T(8,128)(2,1)} %param.3, bf16[16,2,32,1792,1]{2,0,1,3,4:T(8,128)(2,1)} %bitcast.287), kind=kOutput, calls=%fused_computation.15 | convolution fusion | flops 411041792 | bytes 10551296 | tf_op jit(solution)/shard_map/fcrs,fdvs->cdfvr/dot_general | solution.py:41
  334.3 14.6 %all_to_all.150 = bf16[8,2,3584]{2,1,0:T(2,128)(2,1)S(1)} all-to-all(bf16[8,2,3584]{2,1,0:T(2,128)(2,1)S(1)} %reshape.428), channel_id=1, replica_groups=mesh['freq'=8,'rec'=32] {'freq'}, dimensions={0} | all-to-all | bytes 229376 | tf_op jit(solution)/shard_map/all_to_all | solution.py:70
  350.4 10.5 %all_to_all.151 = bf16[8,2,3584]{2,1,0:T(2,128)(2,1)S(1)} all-to-all(bf16[8,2,3584]{2,1,0:T(2,128)(2,1)S(1)} %reshape.430), channel_id=1, replica_groups=mesh['freq'=8,'rec'=32] {'freq'}, dimensions={0} | all-to-all | bytes 229376 | tf_op jit(solution)/shard_map/all_to_all | solution.py:54
  366.9 19.8 %reshape.432 = bf16[32,2,28672]{2,1,0:T(2,128)(2,1)} reshape(bf16[32,16,2,32,56]{4,3,2,1,0:T(8,128)(2,1)} %stack.31) | data formatting | bytes 7340032
  386.7 88.9 %all_to_all.152 = bf16[32,2,28672]{2,1,0:T(2,128)(2,1)} all-to-all(bf16[32,2,28672]{2,1,0:T(2,128)(2,1)} %reshape.432), channel_id=1, replica_groups=mesh['freq'=8,'rec'=32] {'rec'}, dimensions={0} | all-to-all | bytes 7340032 | tf_op jit(solution)/shard_map/all_to_all | solution.py:58
  475.6 21.2 %reshape.433 = bf16[32,16,2,32,56]{4,3,2,1,0:T(8,128)(2,1)} reshape(bf16[32,2,28672]{2,1,0:T(2,128)(2,1)} %all_to_all.152) | data formatting | bytes 7340032
  496.8 20.0 %copy.116 = bf16[16,2,32,32,56]{4,3,2,1,0:T(8,128)(2,1)} copy(bf16[16,2,32,32,56]{4,2,1,0,3:T(8,128)(2,1)} %bitcast.266) | data formatting | bytes 7340032 | tf_op jit(solution)/shard_map/reshape | solution.py:57
  516.8 14.3 %reshape.413 = bf16[16,2,32,1792,1]{3,2,1,0,4:T(8,128)(2,1)} reshape(bf16[16,2,32,32,56]{4,3,2,1,0:T(8,128)(2,1)} %copy.116) | data formatting | bytes 7340032 | tf_op jit(solution)/shard_map/reshape | solution.py:57
  531.0 7.4 %fusion.22 = f32[2,2,16,32,56]{4,3,0,1,2:T(8,128)S(1)} fusion(bf16[16,2,56,1792]{3,2,1,0:T(8,128)(2,1)} %param.3, bf16[16,2,32,1792,1]{3,2,1,0,4:T(8,128)(2,1)} %reshape.413), kind=kOutput, calls=%fused_computation.14 | convolution fusion | flops 411041792 | bytes 10551296 | tf_op jit(solution)/shard_map/fcrs,fdvs->cdfvr/dot_general | solution.py:41
  539.1 10.6 %all_to_all.153 = bf16[8,2,3584]{2,1,0:T(2,128)(2,1)S(1)} all-to-all(bf16[8,2,3584]{2,1,0:T(2,128)(2,1)S(1)} %reshape.434), channel_id=1, replica_groups=mesh['freq'=8,'rec'=32] {'freq'}, dimensions={0} | all-to-all | bytes 229376 | tf_op jit(solution)/shard_map/all_to_all | solution.py:61
  551.3 10.7 %all_to_all.154 = bf16[8,2,3584]{2,1,0:T(2,128)(2,1)S(1)} all-to-all(bf16[8,2,3584]{2,1,0:T(2,128)(2,1)S(1)} %reshape.436), channel_id=1, replica_groups=mesh['freq'=8,'rec'=32] {'freq'}, dimensions={0} | all-to-all | bytes 229376 | tf_op jit(solution)/shard_map/all_to_all | solution.py:65
  564.0 85.8 %all-gather.5.cloned.1.call-done = bf16[16,2,32,1792]{2,0,1,3:T(8,128)(2,1)} async-done(((bf16[16,2,32,56]{2,0,1,3:T(8,128)(2,1)}), bf16[16,2,32,1792]{2,0,1,3:T(8,128)(2,1)}) %all-gather.5.cloned.1.call-update) | async-done | bytes 3670032 | tf_op jit(solution)/shard_map/all_gather | solution.py:68
  649.8 15.1 %fusion.12 = f32[2,2,16,32,56]{4,3,2,1,0:T(8,128)S(1)} fusion(bf16[16,2,32,1792,1]{2,0,1,3,4:T(8,128)(2,1)} %bitcast.288, bf16[16,2,56,1792]{3,2,1,0:T(8,128)(2,1)} %param.3), kind=kOutput, calls=%fused_computation.12 | convolution fusion | flops 411041792 | bytes 10551296 | tf_op jit(solution)/shard_map/fcrs,fdvs->cdfvr/dot_general | solution.py:41
  (76 shorter events, 46.7 us)
Async XLA Ops:
  50.1 92.7 %all-to-all-start.1 = ((bf16[32,2,28672]{2,1,0:T(2,128)(2,1)}), bf16[32,2,28672]{2,1,0:T(2,128)(2,1)}, u32[]{:S(2)}, u32[]{:S(2)}) async-start(bf16[32,2,28672]{2,1,0:T(2,128)(2,1)} %reshape.422), calls=%async_computation.1 | async-start | bytes 7340032 | tf_op jit(solution)/shard_map/all_to_all | solution.py:58
  198.3 20.6 %copy-start.1 = (s32[56,4]{0,1:T(4,128)S(1)}, s32[56,4]{0,1:T(4,128)}, u32[]{:S(2)}) copy-start(s32[56,4]{0,1:T(4,128)} %param.5) | copy-start | bytes 2692
  207.0 11.4 %all-to-all-start.2 = ((bf16[8,2,3584]{2,1,0:T(2,128)(2,1)}), bf16[8,2,3584]{2,1,0:T(2,128)(2,1)S(1)}, u32[]{:S(2)}, u32[]{:S(2)}) async-start(bf16[8,2,3584]{2,1,0:T(2,128)(2,1)} %reshape.424), calls=%async_computation.2 | async-start | bytes 229376 | tf_op jit(solution)/shard_map/all_to_all | solution.py:61
  210.4 107.9 %all-gather.3.cloned.1.call-start = ((), (), s32[]{:S(2)}) async-start(), calls=%async_computation.10 | async-start | bytes 15138816 | tf_op jit(solution)/shard_map/all_gather | solution.py:68
  232.4 417.4 %all-gather.5.cloned.1.call-start = ((), (), s32[]{:S(2)}) async-start(), calls=%async_computation.11 | async-start | bytes 15138816 | tf_op jit(solution)/shard_map/all_gather | solution.py:68
  318.3 31.1 %copy-start = (f32[56,4,256]{2,1,0:T(4,128)S(1)}, f32[56,4,256]{2,1,0:T(4,128)}, u32[]{:S(2)}) copy-start(f32[56,4,256]{2,1,0:T(4,128)} %param.4) | copy-start | bytes 688132
  666.2 14.8 %all-to-all-start.9 = ((bf16[8,2,3584]{2,1,0:T(2,128)(2,1)}), bf16[8,2,3584]{2,1,0:T(2,128)(2,1)S(1)}, u32[]{:S(2)}, u32[]{:S(2)}) async-start(bf16[8,2,3584]{2,1,0:T(2,128)(2,1)} %reshape.438), calls=%async_computation.9 | async-start | bytes 229376 | tf_op jit(solution)/shard_map/all_to_all | solution.py:70
Sparse Core Ops, SparseCore 0:
  232.6 85.6 all-gather.2
  564.1 85.6 all-gather.4
